TPU v7x, 32 devices: a whole 2x2x4 slice. The times are simulated.
32 devices in a mesh: groups: 2 (over x), ep: 4 (over y, core), rep: 4 (over z).
Axes of the slice: x: 2, y: 2, z: 4, core: 2. Of those that a mesh axis runs over, the one named last changes fastest.
Arguments:
- prompt_hidden: bfloat16 [8, 96, 2048], P('groups', 'ep'), parts along dimension 0, may hold values from -6 to 6
- decode_hidden: bfloat16 [64, 8, 2048], P(('groups', 'ep'), 'rep'), parts along dimension 0, may hold values from -6 to 6
- queries: bfloat16 [64, 8, 2048], P(('groups', 'ep'), None, 'rep'), parts along dimension 0, may hold values from -128 to 128
- attn_gain: float32 [2048], replicated, may hold values from 0.1 to 1.9
- key_value_weight: bfloat16 [2048, 1024], P(None, 'rep'), may hold values from -0.125 to 0.125
- out_weight: bfloat16 [2048, 2048], P('rep'), may hold values from -0.5 to 0.5
- moe_gain: float32 [2048], replicated, may hold values from 0.1 to 1.9
- gate_weight: bfloat16 [16, 2048, 768], P(('ep', 'rep')), may hold values from -0.125 to 0.125
- up_weight: bfloat16 [16, 2048, 768], P(('ep', 'rep')), may hold values from -0.125 to 0.125
- down_weight: bfloat16 [16, 768, 2048], P(('ep', 'rep')), may hold values from -0.21875 to 0.21875
- expert_table: int32 [151936], replicated, may hold values from 0 to 15, as said below
- token_ids: int32 [32, 8], P('ep', 'rep'), may hold values from 0 to 151935, as said below
- prompt_lengths: int32 [8], P('groups'), parts along dimension 0, may hold values from 1 to 96, 240 in all
Outputs:
- layer_out: bfloat16 [64, 8, 2048], P(('groups', 'ep'), 'rep'), parts along dimension 0
There are 2 independent parts, one for each index of `groups`. A program takes and returns all parts, laid end to end along the dimension named above; an argument that names none is the same for every part. Nothing has to cross between parts.
Inputs may be any that keep to these rules, and one draw needn't show every extreme that they name: `expert_table`: each expert is the value of exactly 9496 entries. `token_ids`: a device holds the 8 sequences of its index of ep at 8 // 4 steps of its index of rep; of these tokens at most 2 go to one expert; in every draw one expert receives exactly 2 from every device. `prompt_lengths`: the lengths of a group sum to 240 and the longest is 96.
All inputs are finite; a program needn't handle non-finite values.
Results may differ from a plain program's by a relative error of at most 0.017.
The roundings to bfloat16 on the way count: a program that leaves them out, or rounds other values in their place, can miss the bound.
Values may be sent and summed in bfloat16 or wider, within the bound.
No kernel may reach another device: no remote copies, remote signals or barrier semaphores. Data moves between devices by JAX's collectives and lax.ppermute only.
A program may use at most 128 MiB of HBM per device.

v0:
```python
import math
import jax
import jax.numpy as jnp
from jax import lax
from jax.sharding import PartitionSpec as P

HEAD_DIM = 128
QUERY_HEADS = 16
KEY_VALUE_HEADS = 4
GROUP_PROMPTS = 4
CAP = 2
EPS = 1e-06
THETA = 1000000.0


def swapped(block, axis, bit):
    count = lax.axis_size(axis)
    route = []
    for low in range(count):
        high = low | 1 << bit
        if high != low and high < count:
            route += [(low, high), (high, low)]
    return lax.ppermute(block, axis, route)


def rms_scale(hidden, gain_vec):
    widened = hidden.astype(jnp.float32)
    mean_sq = jnp.mean(widened * widened, axis=-1, keepdims=True)
    return widened * lax.rsqrt(mean_sq + EPS) * gain_vec


def rotate(vectors, positions):
    half_dim = vectors.shape[-1] // 2
    inverse_freq = jnp.exp(
        jnp.arange(half_dim, dtype=jnp.float32) * (-2.0 * math.log(THETA) / vectors.shape[-1])
    )
    angles = positions[..., None] * inverse_freq
    cosine = jnp.cos(angles)
    sine_part = jnp.sin(angles)
    first_half = vectors[..., :half_dim]
    second_half = vectors[..., half_dim:]
    return jnp.concatenate(
        [
            first_half * cosine - second_half * sine_part,
            second_half * cosine + first_half * sine_part,
        ],
        axis=-1,
    )


def expert_apply(tokens, gate_weight, up_weight, down_weight):
    flat_rows = tokens.reshape(-1, tokens.shape[-1])
    gate_proj = jnp.dot(flat_rows, gate_weight[0], preferred_element_type=jnp.float32)
    up_proj = jnp.dot(flat_rows, up_weight[0], preferred_element_type=jnp.float32)
    hidden = (jax.nn.silu(gate_proj) * up_proj).astype(jnp.bfloat16)
    return (
        jnp.dot(hidden, down_weight[0], preferred_element_type=jnp.float32)
        .astype(jnp.bfloat16)
        .reshape(tokens.shape)
    )


def local(
    prompt_hidden,
    decode_hidden,
    queries,
    attn_gain,
    key_value_weight,
    out_weight,
    moe_gain,
    gate_weight,
    up_weight,
    down_weight,
    expert_table,
    token_ids,
    prompt_lengths,
):
    full_hidden = lax.all_gather(decode_hidden, "rep", axis=1, tiled=True)
    sequences_local, steps_total, model_width = full_hidden.shape
    prompt_length_local = prompt_hidden.shape[1]
    qh_dev = queries.shape[2] // HEAD_DIM
    group_count = QUERY_HEADS // KEY_VALUE_HEADS
    ep_count = lax.axis_size("ep")
    rep_count = lax.axis_size("rep")
    ep_index = lax.axis_index("ep")
    rep_index = lax.axis_index("rep")
    seq_total = sequences_local * ep_count
    samples = seq_total // GROUP_PROMPTS
    score_scale = HEAD_DIM ** (-0.5)
    step_rows = steps_total // rep_count
    blocks = key_value_weight.shape[1] // HEAD_DIM

    def own_columns(hidden, positions):
        leading = hidden.shape[:-1]
        normed = rms_scale(hidden, attn_gain).astype(jnp.bfloat16)
        projected = jnp.dot(
            normed.reshape(-1, model_width), key_value_weight, preferred_element_type=jnp.float32
        )
        projected = projected.reshape(leading + (blocks, HEAD_DIM))
        block_ids = rep_index * blocks + jnp.arange(blocks, dtype=jnp.int32)
        is_key = (block_ids % 2 == 0)[:, None]
        turned = rotate(projected, positions[..., None])
        return (
            jnp.where(is_key, turned, projected)
            .astype(jnp.bfloat16)
            .reshape(leading + (blocks * HEAD_DIM,))
        )

    key_pos = ep_index * prompt_length_local + jnp.arange(prompt_length_local, dtype=jnp.int32)
    prompt_pos = jnp.broadcast_to(
        key_pos.astype(jnp.float32)[None, :], (GROUP_PROMPTS, prompt_length_local)
    )
    own_seqs = ep_index * sequences_local + jnp.arange(sequences_local, dtype=jnp.int32)
    own_prompt = own_seqs // samples
    own_lengths = jnp.take(prompt_lengths, own_prompt)
    decode_pos = (
        own_lengths[:, None].astype(jnp.float32)
        + jnp.arange(steps_total, dtype=jnp.float32)[None, :]
    )
    prompt_part = own_columns(prompt_hidden, prompt_pos)
    decode_part = own_columns(full_hidden, decode_pos)
    prompt_hot = own_prompt[:, None] == jnp.arange(GROUP_PROMPTS, dtype=jnp.int32)[None, :]
    if blocks == 1:
        partner_prompt, partner_decode = swapped((prompt_part, decode_part), "rep", 0)
        holds_key = rep_index % 2 == 0
        prompt_columns = jnp.where(
            holds_key,
            jnp.concatenate([prompt_part, partner_prompt], axis=2),
            jnp.concatenate([partner_prompt, prompt_part], axis=2),
        )
        decode_columns = jnp.where(
            holds_key,
            jnp.concatenate([decode_part, partner_decode], axis=2),
            jnp.concatenate([partner_decode, decode_part], axis=2),
        )
        heads_here = 1
        head_base = rep_index // 2
    else:
        prompt_columns = prompt_part
        decode_columns = decode_part
        heads_here = blocks // 2
        head_base = rep_index * heads_here
    prompt_key_value = prompt_columns.reshape(
        GROUP_PROMPTS, prompt_length_local, heads_here, 2, HEAD_DIM
    )
    decode_key_value = decode_columns.reshape(sequences_local, steps_total, heads_here, 2, HEAD_DIM)
    prompt_keys = prompt_key_value[:, :, :, 0, :]
    prompt_values = prompt_key_value[:, :, :, 1, :]
    decode_keys = decode_key_value[:, :, :, 0, :]
    decode_values = decode_key_value[:, :, :, 1, :]
    query_matrix = queries.reshape(sequences_local, steps_total, qh_dev, HEAD_DIM)
    head_pick = (
        rep_index * qh_dev + jnp.arange(qh_dev, dtype=jnp.int32)
    ) // group_count - head_base
    own_keys = jnp.take(decode_keys, head_pick, axis=2)
    own_values = jnp.take(decode_values, head_pick, axis=2)
    self_scores = (
        jnp.einsum("sthd,suhd->sthu", query_matrix, own_keys, preferred_element_type=jnp.float32)
        * score_scale
    )
    self_mask = (
        jnp.arange(steps_total, dtype=jnp.int32)[None, :]
        <= jnp.arange(steps_total, dtype=jnp.int32)[:, None]
    )[None, :, None, :]
    self_scores = jnp.where(self_mask, self_scores, -1e30)
    self_top = jnp.max(self_scores, axis=-1)
    start_weights = jnp.where(self_mask, jnp.exp(self_scores - self_top[..., None]), 0.0)
    row_top = self_top
    row_total = jnp.sum(start_weights, axis=-1)
    weighted = jnp.einsum(
        "sthu,suhd->sthd",
        start_weights.astype(jnp.bfloat16),
        own_values,
        preferred_element_type=jnp.float32,
    )
    piece_keys = jnp.take(lax.all_gather(prompt_keys, "ep", axis=1, tiled=True), head_pick, axis=2)
    piece_values = jnp.take(
        lax.all_gather(prompt_values, "ep", axis=1, tiled=True), head_pick, axis=2
    )
    piece_len = piece_keys.shape[1]
    valid = jnp.arange(piece_len, dtype=jnp.int32)[None, :] < prompt_lengths[:, None]
    key_mask = prompt_hot[:, None, None, :, None] & valid[None, None, None, :, :]
    scores = (
        jnp.einsum("sthd,pnhd->sthpn", query_matrix, piece_keys, preferred_element_type=jnp.float32)
        * score_scale
    )
    scores = jnp.where(key_mask, scores, -1e30)
    new_top = jnp.maximum(row_top, jnp.max(scores, axis=(-2, -1)))
    decay = jnp.exp(row_top - new_top)
    weights = jnp.where(key_mask, jnp.exp(scores - new_top[..., None, None]), 0.0)
    weighted = weighted * decay[..., None] + jnp.einsum(
        "sthpn,pnhd->sthd",
        weights.astype(jnp.bfloat16),
        piece_values,
        preferred_element_type=jnp.float32,
    )
    row_top, row_total, weighted = (
        new_top,
        row_total * decay + jnp.sum(weights, axis=(-2, -1)),
        weighted,
    )
    attended = weighted / row_total[..., None]
    heads_out = attended.reshape(sequences_local, steps_total, qh_dev * HEAD_DIM).astype(
        jnp.bfloat16
    )
    by_step = jnp.swapaxes(heads_out, 0, 1)
    attn_sum = jnp.swapaxes(
        lax.psum_scatter(
            jnp.dot(
                by_step.reshape(-1, by_step.shape[-1]),
                out_weight,
                preferred_element_type=jnp.float32,
            )
            .reshape(step_rows * lax.axis_size("rep"), sequences_local, model_width)
            .astype(jnp.bfloat16),
            "rep",
            scatter_dimension=0,
            tiled=True,
        ).astype(jnp.float32),
        0,
        1,
    )
    attn_mixed = (decode_hidden.astype(jnp.float32) + attn_sum).astype(jnp.bfloat16)
    row_count = sequences_local * step_rows
    normed = rms_scale(attn_mixed, moe_gain).astype(jnp.bfloat16).reshape(row_count, model_width)
    chosen = jnp.take(expert_table, token_ids.reshape(row_count))
    device_count = ep_count * rep_count
    slot_total = device_count * CAP
    same_expert = chosen[:, None] == chosen[None, :]
    before = jnp.arange(row_count)[None, :] < jnp.arange(row_count)[:, None]
    slot_rank = jnp.sum((same_expert & before).astype(jnp.int32), axis=1)
    destination = chosen * CAP + slot_rank
    send_pick = (jnp.arange(slot_total, dtype=jnp.int32)[:, None] == destination[None, :]).astype(
        jnp.bfloat16
    )
    outgoing = (
        jnp.dot(send_pick, normed, preferred_element_type=jnp.float32)
        .astype(jnp.bfloat16)
        .reshape(device_count, CAP, model_width)
    )
    served = expert_apply(
        lax.all_to_all(outgoing, ("ep", "rep"), split_axis=0, concat_axis=0, tiled=True),
        gate_weight,
        up_weight,
        down_weight,
    )
    returned = lax.all_to_all(served, ("ep", "rep"), split_axis=0, concat_axis=0, tiled=True)
    moe_out = lax.dot_general(
        send_pick,
        returned.reshape(slot_total, model_width),
        (((0,), (0,)), ((), ())),
        preferred_element_type=jnp.float32,
    )
    layer_out = (
        attn_mixed.astype(jnp.float32) + moe_out.reshape(sequences_local, step_rows, model_width)
    ).astype(jnp.bfloat16)
    return layer_out


def solution(mesh):
    placed = (
        P("groups", "ep", None),
        P(("groups", "ep"), "rep", None),
        P(("groups", "ep"), None, "rep"),
        P(),
        P(None, "rep"),
        P("rep", None),
        P(),
        P(("ep", "rep"), None, None),
        P(("ep", "rep"), None, None),
        P(("ep", "rep"), None, None),
        P(),
        P("ep", "rep"),
        P("groups"),
    )
    return jax.shard_map(
        local,
        mesh=mesh,
        in_specs=placed,
        out_specs=P(("groups", "ep"), "rep", None),
        check_vma=False,
    )
```

profile of v0, /device:TPU:0, one launch (start us, length us, event | category | flops | bytes accessed | tf_op | source)
XLA Modules:
  0.0 108.6 jit_solution(1051078798896082952)
XLA Ops:
  6.5 0.0 copy-start
  6.5 0.0 copy-start.4
  6.5 0.0 reduce-scatter.2.cloned.1.call-start
  6.6 0.9 iota_compare_fusion.5
  7.5 1.3 %gather_fusion = s32[8]{0:T(128)S(1)} fusion(s32[4]{0:T(128)} %param.29, s32[1024]{0:T(1024)S(1)} %pad_clamp_fusion.1), kind=kCustom, calls=%fused_computation | custom fusion | bytes 96 | tf_op jit(solution)/shard_map/jit(_take)/gather | solution.py:115
  8.8 2.3 %copy.120 = bf16[256,2048]{1,0:T(8,128)(2,1)} copy(bf16[256,2048]{0,1:T(8,128)(2,1)} %bitcast.124) | data formatting | bytes 2097152 | tf_op jit(solution)/shard_map/dot_general | solution.py:96
  11.1 0.0 copy-start.7
  11.1 0.9 copy.92
  12.0 15.7 %all_gather.9 = bf16[8,8,2048]{2,0,1:T(8,128)(2,1)S(1)} all-gather(bf16[8,2,2048]{2,0,1:T(8,128)(2,1)S(1)} %copy.92), channel_id=1, replica_groups=mesh['groups'=2,'ep'=4,'rep'=4] {'rep'}, dimensions={1}, use_global_device_ids=true | all-gather | bytes 327680 | tf_op jit(solution)/shard_map/all_gather | solution.py:78
  27.7 0.1 fusion.31
  27.9 0.2 multiply_cosine_fusion.1
  28.1 0.0 copy-done.4
  28.1 1.7 %fusion.48 = f32[8,8,2,128]{3,0,2,1:T(8,128)S(1)} fusion(bf16[2,128,2048,1]{2,1,0,3:T(8,128)(2,1)} %bitcast.122, bf16[8,8,2048]{2,0,1:T(8,128)(2,1)S(1)} %all_gather.9, f32[2048]{0:T(1024)S(1)} %copy-done.4, f32[8,8]{0,1:T(8,128)S(1)} %add_rsqrt_fusion), kind=kOutput, calls=%fused_computation.53 | convolution fusion | flops 67633152 | bytes 1384704 | tf_op jit(solution)/shard_map/dot_general | solution.py:96
  29.7 0.1 multiply_subtract_fusion.1
  29.8 0.1 fusion.83
  30.0 0.1 multiply_cosine_fusion
  30.1 1.1 %fusion.28 = f32[4,24]{1,0:T(4,128)S(1)} fusion(bf16[4,24,2048]{2,1,0:T(8,128)(2,1)} %param.17), kind=kLoop, calls=%fused_computation.31 | loop fusion | flops 589728 | bytes 393600 | tf_op jit(solution)/shard_map/reduce_sum | solution.py:28
  31.3 1.8 %fusion.37 = f32[4,24,2,128]{3,1,2,0:T(8,128)S(1)} fusion(bf16[2,128,2048,1]{2,1,0,3:T(8,128)(2,1)} %bitcast.123, bf16[4,24,2048]{2,1,0:T(8,128)(2,1)} %param.17, f32[2048]{0:T(1024)S(1)} %copy-done.4, f32[4,24]{1,0:T(4,128)S(1)} %add_rsqrt_fusion.1), kind=kOutput, calls=%fused_computation.43 | convolution fusion | flops 101449728 | bytes 1548672 | tf_op jit(solution)/shard_map/dot_general | solution.py:96
  33.1 0.0 copy-start.1
  33.1 0.1 multiply_subtract_fusion
  33.2 0.1 fusion.81
  33.4 5.5 %all-gather = bf16[4,96,1,1,128]{4,1,3,0,2:T(8,128)(2,1)S(1)} all-gather(bf16[4,24,1,1,128]{4,1,3,0,2:T(8,128)(2,1)S(1)} %get-tuple-element.16), channel_id=2, replica_groups=mesh['groups'=2,'ep'=4,'rep'=4] {'ep'}, dimensions={1}, use_global_device_ids=true | all-gather | bytes 122880 | tf_op jit(solution)/shard_map/all_gather | solution.py:176
  38.8 0.0 copy-done.7
  38.8 0.3 fusion.105
  39.1 0.1 fusion.61
  39.2 0.1 broadcast_and_fusion
  39.3 0.6 fusion.104
  39.8 0.0 copy-start.6
  39.8 0.3 fusion.34
  40.1 0.0 copy-start.2
  40.1 0.0 copy-start.5
  40.2 5.3 %all-gather.1 = bf16[4,96,1,1,128]{4,1,3,0,2:T(8,128)(2,1)S(1)} all-gather(bf16[4,24,1,1,128]{4,1,3,0,2:T(8,128)(2,1)S(1)} %get-tuple-element.15), channel_id=3, replica_groups=mesh['groups'=2,'ep'=4,'rep'=4] {'ep'}, dimensions={1}, use_global_device_ids=true | all-gather | bytes 122880 | tf_op jit(solution)/shard_map/all_gather | solution.py:178
  45.5 0.3 convolution_bitcast_fusion
  45.8 0.3 fusion.25
  46.1 0.0 copy-done.1
  46.1 1.2 %convolution_convert_fusion = bf16[8,8,2048]{2,1,0:T(8,128)(2,1)} fusion(bf16[512,2048]{1,0:T(8,128)(2,1)S(1)} %copy-done.1, bf16[8,8,512]{2,0,1:T(8,128)(2,1)S(1)} %fusion.25), kind=kOutput, calls=%fused_computation.8 | convolution fusion | flops 134348800 | bytes 2424832 | tf_op jit(solution)/shard_map/dot_general | solution.py:209
  47.3 0.0 reduce-scatter.2.cloned.1.call-update
  47.3 0.0 copy-done.6
  47.3 0.1 copy.107
  47.4 0.1 reshape.383
  47.5 0.1 reshape.382
  47.6 1.5 %gather_fusion.1 = s32[16]{0:T(128)S(1)} fusion(s32[151936]{0:T(1024)} %param.27, s32[1024]{0:T(1024)S(1)} %pad_clamp_fusion), kind=kCustom, calls=%fused_computation.1 | custom fusion | bytes 192 | tf_op jit(solution)/shard_map/jit(_take)/gather | solution.py:226
  49.1 0.2 convert_reduce_fusion
  49.2 19.7 %reduce-scatter.2.cloned.1.call-done = bf16[2,8,2048]{2,1,0:T(8,128)(2,1)} async-done(((bf16[8,8,2048]{2,1,0:T(8,128)(2,1)}), bf16[2,8,2048]{2,1,0:T(8,128)(2,1)}) %reduce-scatter.2.cloned.1.call-update) | async-done | bytes 65552 | tf_op jit(solution)/shard_map/reduce_scatter | solution.py:208
  69.0 0.0 copy-done.2
  69.0 1.0 fusion.57
  70.0 0.0 copy-done.5
  70.0 0.9 fusion.59
  70.9 0.1 copy.109
  71.0 0.2 convolution_convert_fusion.1
  71.2 0.1 reshape.385
  71.3 10.7 %all_to_all.10 = bf16[16,2,2048]{2,1,0:T(2,128)(2,1)} all-to-all(bf16[16,2,2048]{2,1,0:T(2,128)(2,1)S(1)} %reshape.385), channel_id=1, replica_groups=mesh['groups'=2,'ep'=4,'rep'=4] {'ep','rep'}, dimensions={0} | all-to-all | bytes 262144 | tf_op jit(solution)/shard_map/all_to_all | solution.py:242
  81.9 1.0 reshape.386
  82.9 3.1 %fusion.4 = f32[32,768]{1,0:T(8,128)} fusion(bf16[32,2048]{1,0:T(8,128)(2,1)S(1)} %reshape.386, bf16[1,2048,768]{2,1,0:T(8,128)(2,1)} %param.24), kind=kOutput, calls=%fused_computation.6 | convolution fusion | flops 100663296 | bytes 3375104 | tf_op jit(solution)/shard_map/dot_general | solution.py:53
  86.0 0.0 copy-done
  86.0 3.2 %fusion.6 = bf16[32,2048]{1,0:T(8,128)(2,1)S(1)} fusion(bf16[1,768,2048]{2,1,0:T(8,128)(2,1)S(1)} %copy-done, bf16[32,2048]{1,0:T(8,128)(2,1)S(1)} %reshape.386, bf16[1,2048,768]{2,1,0:T(8,128)(2,1)} %param.25, f32[32,768]{1,0:T(8,128)} %fusion.4), kind=kOutput, calls=%fused_computation.9 | convolution fusion | flops 201539584 | bytes 6651904 | tf_op jit(solution)/shard_map/dot_general | solution.py:57
  89.2 0.8 reshape.387
  90.0 3.5 %all-to-all-start.1 = ((bf16[16,2,2048]{2,1,0:T(2,128)(2,1)}), bf16[16,2,2048]{2,1,0:T(2,128)(2,1)S(1)}, u32[]{:S(2)}, u32[]{:S(2)}) async-start(bf16[16,2,2048]{2,1,0:T(2,128)(2,1)} %reshape.387), calls=%async_computation.2 | async-start | bytes 262144 | tf_op jit(solution)/shard_map/all_to_all | solution.py:247
  93.5 0.1 iota_compare_fusion.3
  93.6 7.3 %all-to-all-done.1 = bf16[16,2,2048]{2,1,0:T(2,128)(2,1)S(1)} async-done(((bf16[16,2,2048]{2,1,0:T(2,128)(2,1)}), bf16[16,2,2048]{2,1,0:T(2,128)(2,1)S(1)}, u32[]{:S(2)}, u32[]{:S(2)}) %all-to-all-start.1) | async-done | bytes 131104 | tf_op jit(solution)/shard_map/all_to_all | solution.py:247
  100.9 0.1 reshape.424
  100.9 0.0 copy-done.3
  100.9 0.1 fusion.9
  101.1 0.7 copy.111
  (28 shorter events, 0.2 us)
Async XLA Ops:
  6.5 79.5 %copy-start = (bf16[1,768,2048]{2,1,0:T(8,128)(2,1)S(1)}, bf16[1,768,2048]{2,1,0:T(8,128)(2,1)}, u32[]{:S(2)}) copy-start(bf16[1,768,2048]{2,1,0:T(8,128)(2,1)} %param.26) | copy-start | bytes 9437188
  6.5 21.5 %copy-start.4 = (f32[2048]{0:T(1024)S(1)}, f32[2048]{0:T(1024)}, u32[]{:S(2)}) copy-start(f32[2048]{0:T(1024)} %param.20) | copy-start | bytes 24580
  6.5 62.4 %reduce-scatter.2.cloned.1.call-start = ((), (), s32[]{:S(2)}) async-start(), calls=%async_computation.3 | async-start | bytes 327680 | tf_op jit(solution)/shard_map/reduce_scatter | solution.py:208
  11.1 27.7 %copy-start.7 = (bf16[8,8,512]{2,1,0:T(8,128)(2,1)S(1)}, bf16[8,8,512]{2,1,0:T(8,128)(2,1)}, u32[]{:S(2)}) copy-start(bf16[8,8,512]{2,1,0:T(8,128)(2,1)} %param.19) | copy-start | bytes 196612
  33.1 12.9 %copy-start.1 = (bf16[512,2048]{1,0:T(8,128)(2,1)S(1)}, bf16[512,2048]{1,0:T(8,128)(2,1)}, u32[]{:S(2)}) copy-start(bf16[512,2048]{1,0:T(8,128)(2,1)} %param.22) | copy-start | bytes 6291460
  39.8 7.5 %copy-start.6 = (s32[8,2]{0,1:T(2,128)S(1)}, s32[8,2]{0,1:T(2,128)}, u32[]{:S(2)}) copy-start(s32[8,2]{0,1:T(2,128)} %param.28) | copy-start | bytes 196
  40.1 28.9 %copy-start.2 = (bf16[8,2,2048]{2,1,0:T(2,128)(2,1)S(1)}, bf16[8,2,2048]{2,1,0:T(2,128)(2,1)}, u32[]{:S(2)}) copy-start(bf16[8,2,2048]{2,1,0:T(2,128)(2,1)} %param.18) | copy-start | bytes 196612
  40.1 29.8 %copy-start.5 = (f32[2048]{0:T(1024)S(1)}, f32[2048]{0:T(1024)}, u32[]{:S(2)}) copy-start(f32[2048]{0:T(1024)} %param.23) | copy-start | bytes 24580
  86.0 14.9 %copy-start.3 = (bf16[2,8,2048]{2,1,0:T(8,128)(2,1)S(1)}, bf16[2,8,2048]{2,1,0:T(8,128)(2,1)}, u32[]{:S(2)}) copy-start(bf16[2,8,2048]{2,1,0:T(8,128)(2,1)} %reduce-scatter.2.cloned.1.call-done) | copy-start | bytes 196612
  90.0 10.9 %all-to-all-start.1 = ((bf16[16,2,2048]{2,1,0:T(2,128)(2,1)}), bf16[16,2,2048]{2,1,0:T(2,128)(2,1)S(1)}, u32[]{:S(2)}, u32[]{:S(2)}) async-start(bf16[16,2,2048]{2,1,0:T(2,128)(2,1)} %reshape.387), calls=%async_computation.2 | async-start | bytes 262144 | tf_op jit(solution)/shard_map/all_to_all | solution.py:247
Sparse Core Ops, SparseCore 0:
  47.4 21.5 reduce-scatter.1
where the time goes:
time: 109 us
  blocking collectives  37.1 us (34%)
  waiting for transfers between devices  27 us (25%)
  between operations  13.7 us (13%)
  matrix products  12.7 us (12%)
  local copies, waits for them, and re-layouts  9 us (8%)
  other arithmetic  5.59 us (5%)
  starting transfers between devices  3.51 us (3%)
    reduce_scatter x1, waiting for transfers between devices, local(): lax.psum_scatter(jnp.dot(by_step.reshape(-1, by_step.shape[-1]), out_weig...  19.7 us
    all_gather x1, blocking collectives, local(): full_hidden = lax.all_gather(decode_hidden, 'rep', axis=1, tiled=True)  15.7 us
    all_to_all x1, blocking collectives, local(): lax.all_to_all(outgoing, ('ep', 'rep'), split_axis=0, concat_axis=0, tile...  10.7 us
    all_to_all x1, waiting for transfers between devices, local(): lax.all_to_all(served, ('ep', 'rep'), split_axis=0, concat_axis=0, tiled=...  7.26 us
    all_gather x1, blocking collectives, local(): lax.all_gather(prompt_keys, 'ep', axis=1, tiled=True)  5.46 us
    all_gather x1, blocking collectives, local(): lax.all_gather(prompt_values, 'ep', axis=1, tiled=True)  5.33 us
    all_to_all x1, starting transfers between devices, local(): lax.all_to_all(served, ('ep', 'rep'), split_axis=0, concat_axis=0, tiled=...  3.51 us
    dot_general x2, matrix products, own_columns(): jnp.dot(normed.reshape(-1, model_width), key_value_weight, preferred_elem...  3.51 us
  transfers between devices with their start and end apart: 2, of which 2 were waited for; matrix products, arithmetic and copies ran while one was open for 2% of the time, Pallas kernels for 0%

commit v1 on v0

--- a/solution.py
+++ b/solution.py
@@ -3,6 +3,7 @@
 import jax.numpy as jnp
 from jax import lax
 from jax.sharding import PartitionSpec as P
+from jax.lax import axis_index, axis_size, ppermute
 
 HEAD_DIM = 128
 QUERY_HEADS = 16
@@ -11,6 +12,18 @@
 CAP = 2
 EPS = 1e-06
 THETA = 1000000.0
+
+
+def _name_hubs(across, sheet):
+    prior, e_now = (axis_size(across), axis_index(across))
+    side_arr = sheet.shape[0] // prior
+    z1 = jnp.roll(sheet, -e_now * side_arr, 0)
+    tray = [lax.slice_in_dim(z1, 0, side_arr, axis=0)]
+    for w in range(1, prior):
+        base_arr = lax.slice_in_dim(z1, w * side_arr, (w + 1) * side_arr, axis=0)
+        tray.append(ppermute(base_arr, across, [(at, (at + w) % prior) for at in range(prior)]))
+    frame_out = jnp.concatenate(tray[::-1], 0)
+    return jnp.roll(frame_out, (e_now + 1) * tray[0].shape[0], 0)
 
 
 def swapped(block, axis, bit):
@@ -238,12 +251,7 @@
         .astype(jnp.bfloat16)
         .reshape(device_count, CAP, model_width)
     )
-    served = expert_apply(
-        lax.all_to_all(outgoing, ("ep", "rep"), split_axis=0, concat_axis=0, tiled=True),
-        gate_weight,
-        up_weight,
-        down_weight,
-    )
+    served = expert_apply(_name_hubs(("ep", "rep"), outgoing), gate_weight, up_weight, down_weight)
     returned = lax.all_to_all(served, ("ep", "rep"), split_axis=0, concat_axis=0, tiled=True)
     moe_out = lax.dot_general(
         send_pick,

time: 109 us -> 122 us (1.12)
  starting transfers between devices: 3.51 us -> 21.7 us
  blocking collectives: 37.1 us -> 26.4 us
  waiting for transfers between devices: 27 us -> 32.5 us
    ppermute x0 -> x15, starting transfers between devices: none -> 18.1 us  [_name_hubs(): ppermute(base_arr, across, [(at, (at + w) % prior) for at in range(prior)])]
    all_to_all x1 -> x0, blocking collectives: 10.7 us -> none  [local(): lax.all_to_all(outgoing, ('ep', 'rep'), split_axis=0, concat_axis=0, tile...]
    ppermute x0 -> x15, waiting for transfers between devices: none -> 5.56 us  [_name_hubs(): ppermute(base_arr, across, [(at, (at + w) % prior) for at in range(prior)])]
  transfers between devices with their start and end apart: 2 -> 17, of which waited for: 2 -> 6; matrix products, arithmetic and copies ran while one was open for 2% -> 2% of each run, Pallas kernels for 0% -> 0%
where the time goes in v1:
time: 122 us
  waiting for transfers between devices  32.5 us (27%)
  blocking collectives  26.4 us (22%)
  starting transfers between devices  21.7 us (18%)
  between operations  13.9 us (11%)
  matrix products  12.7 us (10%)
  local copies, waits for them, and re-layouts  8.4 us (7%)
  other arithmetic  6.29 us (5%)
    reduce_scatter x1, waiting for transfers between devices, local(): lax.psum_scatter(jnp.dot(by_step.reshape(-1, by_step.shape[-1]), out_weig...  19.7 us
    ppermute x15, starting transfers between devices, _name_hubs(): ppermute(base_arr, across, [(at, (at + w) % prior) for at in range(prior)])  18.1 us
    all_gather x1, blocking collectives, local(): full_hidden = lax.all_gather(decode_hidden, 'rep', axis=1, tiled=True)  15.7 us
    all_to_all x1, waiting for transfers between devices, local(): lax.all_to_all(served, ('ep', 'rep'), split_axis=0, concat_axis=0, tiled=...  7.26 us
    ppermute x15, waiting for transfers between devices, _name_hubs(): ppermute(base_arr, across, [(at, (at + w) % prior) for at in range(prior)])  5.56 us
    all_gather x1, blocking collectives, local(): lax.all_gather(prompt_keys, 'ep', axis=1, tiled=True)  5.46 us
    all_gather x1, blocking collectives, local(): lax.all_gather(prompt_values, 'ep', axis=1, tiled=True)  5.33 us
    all_to_all x1, starting transfers between devices, local(): lax.all_to_all(served, ('ep', 'rep'), split_axis=0, concat_axis=0, tiled=...  3.51 us
  transfers between devices with their start and end apart: 17, of which 6 were waited for; matrix products, arithmetic and copies ran while one was open for 2% of the time, Pallas kernels for 0%

profile of v1, /device:TPU:0, one launch (start us, length us, event | category | flops | bytes accessed | tf_op | source)
XLA Modules:
  0.0 121.9 jit_solution(8094455138869729478)
XLA Ops:
  6.6 0.9 iota_compare_fusion.5
  7.5 1.3 %gather_fusion = s32[8]{0:T(128)S(1)} fusion(s32[4]{0:T(128)} %param.31, s32[1024]{0:T(1024)S(1)} %pad_clamp_fusion.1), kind=kCustom, calls=%fused_computation | custom fusion | bytes 96 | tf_op jit(solution)/shard_map/jit(_take)/gather | solution.py:128
  8.8 2.3 %copy.120 = bf16[256,2048]{1,0:T(8,128)(2,1)} copy(bf16[256,2048]{0,1:T(8,128)(2,1)} %bitcast.124) | data formatting | bytes 2097152 | tf_op jit(solution)/shard_map/dot_general | solution.py:109
  11.1 0.9 copy.92
  12.0 15.7 %all_gather.9 = bf16[8,8,2048]{2,0,1:T(8,128)(2,1)S(1)} all-gather(bf16[8,2,2048]{2,0,1:T(8,128)(2,1)S(1)} %copy.92), channel_id=1, replica_groups=mesh['groups'=2,'ep'=4,'rep'=4] {'rep'}, dimensions={1}, use_global_device_ids=true | all-gather | bytes 327680 | tf_op jit(solution)/shard_map/all_gather | solution.py:91
  27.7 0.1 fusion.31
  27.8 0.2 multiply_cosine_fusion.1
  28.0 1.7 %fusion.48 = f32[8,8,2,128]{3,0,2,1:T(8,128)S(1)} fusion(bf16[2,128,2048,1]{2,1,0,3:T(8,128)(2,1)} %bitcast.122, bf16[8,8,2048]{2,0,1:T(8,128)(2,1)S(1)} %all_gather.9, f32[2048]{0:T(1024)S(1)} %copy-done.4, f32[8,8]{0,1:T(8,128)S(1)} %add_rsqrt_fusion), kind=kOutput, calls=%fused_computation.53 | convolution fusion | flops 67633152 | bytes 1384704 | tf_op jit(solution)/shard_map/dot_general | solution.py:109
  29.7 0.1 multiply_subtract_fusion.1
  29.8 0.1 fusion.85
  30.0 0.1 multiply_cosine_fusion
  30.1 1.1 fusion.28
  31.3 1.8 %fusion.37 = f32[4,24,2,128]{3,1,2,0:T(8,128)S(1)} fusion(bf16[2,128,2048,1]{2,1,0,3:T(8,128)(2,1)} %bitcast.123, bf16[4,24,2048]{2,1,0:T(8,128)(2,1)} %param.19, f32[2048]{0:T(1024)S(1)} %copy-done.4, f32[4,24]{1,0:T(4,128)S(1)} %add_rsqrt_fusion.1), kind=kOutput, calls=%fused_computation.43 | convolution fusion | flops 101449728 | bytes 1548672 | tf_op jit(solution)/shard_map/dot_general | solution.py:109
  33.1 0.1 multiply_subtract_fusion
  33.2 0.1 fusion.83
  33.3 5.5 %all-gather = bf16[4,96,1,1,128]{4,1,3,0,2:T(8,128)(2,1)S(1)} all-gather(bf16[4,24,1,1,128]{4,1,3,0,2:T(8,128)(2,1)S(1)} %get-tuple-element.32), channel_id=2, replica_groups=mesh['groups'=2,'ep'=4,'rep'=4] {'ep'}, dimensions={1}, use_global_device_ids=true | all-gather | bytes 122880 | tf_op jit(solution)/shard_map/all_gather | solution.py:189
  38.8 0.1 broadcast_and_fusion
  38.9 0.3 fusion.108
  39.2 0.6 fusion.107
  39.7 0.1 fusion.63
  39.8 0.3 fusion.34
  40.2 5.3 %all-gather.1 = bf16[4,96,1,1,128]{4,1,3,0,2:T(8,128)(2,1)S(1)} all-gather(bf16[4,24,1,1,128]{4,1,3,0,2:T(8,128)(2,1)S(1)} %get-tuple-element.31), channel_id=3, replica_groups=mesh['groups'=2,'ep'=4,'rep'=4] {'ep'}, dimensions={1}, use_global_device_ids=true | all-gather | bytes 122880 | tf_op jit(solution)/shard_map/all_gather | solution.py:191
  45.5 0.3 convolution_bitcast_fusion
  45.8 0.3 fusion.25
  46.1 1.2 convolution_convert_fusion
  47.3 0.1 copy.107
  47.4 0.1 reshape.383
  47.4 0.1 reshape.382
  47.6 1.5 %gather_fusion.1 = s32[16]{0:T(128)S(1)} fusion(s32[151936]{0:T(1024)} %param.29, s32[1024]{0:T(1024)S(1)} %pad_clamp_fusion), kind=kCustom, calls=%fused_computation.1 | custom fusion | bytes 192 | tf_op jit(solution)/shard_map/jit(_take)/gather | solution.py:239
  49.1 0.2 convert_reduce_fusion
  49.3 19.7 %reduce-scatter.2.cloned.1.call-done = bf16[2,8,2048]{2,1,0:T(8,128)(2,1)} async-done(((bf16[8,8,2048]{2,1,0:T(8,128)(2,1)}), bf16[2,8,2048]{2,1,0:T(8,128)(2,1)}) %reduce-scatter.2.cloned.1.call-update) | async-done | bytes 65552 | tf_op jit(solution)/shard_map/reduce_scatter | solution.py:221
  68.9 1.0 fusion.59
  69.9 0.9 fusion.61
  70.8 0.1 copy.109
  71.0 0.2 convolution_convert_fusion.1
  71.1 0.1 reshape.385
  71.2 0.3 fusion.58
  71.6 0.1 fusion.105
  71.8 0.1 collective-permute-start.1
  71.9 3.2 %collective-permute-start.2 = (bf16[1,2,2048]{2,1,0:T(2,128)(2,1)S(1)}, bf16[1,2,2048]{2,1,0:T(2,128)(2,1)S(1)}, u32[]{:S(2)}, u32[]{:S(2)}) collective-permute-start(bf16[1,2,2048]{2,1,0:T(2,128)(2,1)S(1)} %get-tuple-element.26), channel_id=1, source_target_pairs={{0,13},{1,14},{2,15},{3,0},{4,1},{5,2},{6,3},{7,4},{8,5},{9,6},{10... | collective-permute-start | bytes 24584 | tf_op jit(solution)/shard_map/ppermute | solution.py:24
  75.1 2.2 %collective-permute-start.4 = (bf16[1,2,2048]{2,1,0:T(2,128)(2,1)S(1)}, bf16[1,2,2048]{2,1,0:T(2,128)(2,1)S(1)}, u32[]{:S(2)}, u32[]{:S(2)}) collective-permute-start(bf16[1,2,2048]{2,1,0:T(2,128)(2,1)S(1)} %get-tuple-element.24), channel_id=1, source_target_pairs={{0,11},{1,12},{2,13},{3,14},{4,15},{5,0},{6,1},{7,2},{8,3},{9,4},{... | collective-permute-start | bytes 24584 | tf_op jit(solution)/shard_map/ppermute | solution.py:24
  77.2 1.3 %collective-permute-start.5 = (bf16[1,2,2048]{2,1,0:T(2,128)(2,1)S(1)}, bf16[1,2,2048]{2,1,0:T(2,128)(2,1)S(1)}, u32[]{:S(2)}, u32[]{:S(2)}) collective-permute-start(bf16[1,2,2048]{2,1,0:T(2,128)(2,1)S(1)} %get-tuple-element.23), channel_id=1, source_target_pairs={{0,10},{1,11},{2,12},{3,13},{4,14},{5,15},{6,0},{7,1},{8,2},{9,3},... | collective-permute-start | bytes 24584 | tf_op jit(solution)/shard_map/ppermute | solution.py:24
  78.5 1.8 %collective-permute-start.6 = (bf16[1,2,2048]{2,1,0:T(2,128)(2,1)S(1)}, bf16[1,2,2048]{2,1,0:T(2,128)(2,1)S(1)}, u32[]{:S(2)}, u32[]{:S(2)}) collective-permute-start(bf16[1,2,2048]{2,1,0:T(2,128)(2,1)S(1)} %get-tuple-element.22), channel_id=1, source_target_pairs={{0,9},{1,10},{2,11},{3,12},{4,13},{5,14},{6,15},{7,0},{8,1},{9,2},... | collective-permute-start | bytes 24584 | tf_op jit(solution)/shard_map/ppermute | solution.py:24
  80.4 0.6 collective-permute-start.7
  81.0 1.9 %collective-permute-start.8 = (bf16[1,2,2048]{2,1,0:T(2,128)(2,1)S(1)}, bf16[1,2,2048]{2,1,0:T(2,128)(2,1)S(1)}, u32[]{:S(2)}, u32[]{:S(2)}) collective-permute-start(bf16[1,2,2048]{2,1,0:T(2,128)(2,1)S(1)} %get-tuple-element.20), channel_id=1, source_target_pairs={{0,7},{1,8},{2,9},{3,10},{4,11},{5,12},{6,13},{7,14},{8,15},{9,0},... | collective-permute-start | bytes 24584 | tf_op jit(solution)/shard_map/ppermute | solution.py:24
  82.9 0.9 collective-permute-start.9
  83.8 0.6 collective-permute-start.10
  84.4 0.4 collective-permute-start.11
  84.8 4.5 %collective-permute-start.12 = (bf16[1,2,2048]{2,1,0:T(2,128)(2,1)S(1)}, bf16[1,2,2048]{2,1,0:T(2,128)(2,1)S(1)}, u32[]{:S(2)}, u32[]{:S(2)}) collective-permute-start(bf16[1,2,2048]{2,1,0:T(2,128)(2,1)S(1)} %get-tuple-element.16), channel_id=1, source_target_pairs={{0,3},{1,4},{2,5},{3,6},{4,7},{5,8},{6,9},{7,10},{8,11},{9,12},{10... | collective-permute-start | bytes 24584 | tf_op jit(solution)/shard_map/ppermute | solution.py:24
  89.4 0.5 collective-permute-start.13
  89.9 0.2 collective-permute-start.14
  90.1 0.1 collective-permute-done.10
  90.2 0.5 collective-permute-done.12
  90.7 3.6 %collective-permute-done.13 = bf16[1,2,2048]{2,1,0:T(2,128)(2,1)S(1)} collective-permute-done((bf16[1,2,2048]{2,1,0:T(2,128)(2,1)S(1)}, bf16[1,2,2048]{2,1,0:T(2,128)(2,1)S(1)}, u32[]{:S(2)}, u32[]{:S(2)}) %collective-permute-start.13) | collective-permute-done | bytes 8224 | tf_op jit(solution)/shard_map/ppermute | solution.py:24
  94.3 1.4 %collective-permute-done.14 = bf16[1,2,2048]{2,1,0:T(2,128)(2,1)S(1)} collective-permute-done((bf16[1,2,2048]{2,1,0:T(2,128)(2,1)S(1)}, bf16[1,2,2048]{2,1,0:T(2,128)(2,1)S(1)}, u32[]{:S(2)}, u32[]{:S(2)}) %collective-permute-start.14) | collective-permute-done | bytes 8224 | tf_op jit(solution)/shard_map/ppermute | solution.py:24
  95.7 0.3 fusion.57
  96.2 3.1 %fusion.4 = f32[32,768]{1,0:T(8,128)} fusion(bf16[32,2048]{1,0:T(8,128)(2,1)S(1)} %reshape.386, bf16[1,2048,768]{2,1,0:T(8,128)(2,1)} %param.26), kind=kOutput, calls=%fused_computation.6 | convolution fusion | flops 100663296 | bytes 3375104 | tf_op jit(solution)/shard_map/dot_general | solution.py:66
  99.3 3.2 %fusion.6 = bf16[32,2048]{1,0:T(8,128)(2,1)S(1)} fusion(bf16[1,768,2048]{2,1,0:T(8,128)(2,1)S(1)} %copy-done, bf16[32,2048]{1,0:T(8,128)(2,1)S(1)} %reshape.386, bf16[1,2048,768]{2,1,0:T(8,128)(2,1)} %param.27, f32[32,768]{1,0:T(8,128)} %fusion.4), kind=kOutput, calls=%fused_computation.9 | convolution fusion | flops 201539584 | bytes 6651904 | tf_op jit(solution)/shard_map/dot_general | solution.py:70
  102.5 0.8 reshape.387
  103.3 3.5 %all-to-all-start = ((bf16[16,2,2048]{2,1,0:T(2,128)(2,1)}), bf16[16,2,2048]{2,1,0:T(2,128)(2,1)S(1)}, u32[]{:S(2)}, u32[]{:S(2)}) async-start(bf16[16,2,2048]{2,1,0:T(2,128)(2,1)} %reshape.387), calls=%async_computation.1 | async-start | bytes 262144 | tf_op jit(solution)/shard_map/all_to_all | solution.py:255
  106.8 0.1 iota_compare_fusion.3
  106.9 7.3 %all-to-all-done = bf16[16,2,2048]{2,1,0:T(2,128)(2,1)S(1)} async-done(((bf16[16,2,2048]{2,1,0:T(2,128)(2,1)}), bf16[16,2,2048]{2,1,0:T(2,128)(2,1)S(1)}, u32[]{:S(2)}, u32[]{:S(2)}) %all-to-all-start) | async-done | bytes 131104 | tf_op jit(solution)/shard_map/all_to_all | solution.py:255
  114.2 0.1 fusion.9
  114.4 0.7 copy.111
  (76 shorter events, 0.7 us)
Async XLA Ops:
  6.5 92.8 %copy-start = (bf16[1,768,2048]{2,1,0:T(8,128)(2,1)S(1)}, bf16[1,768,2048]{2,1,0:T(8,128)(2,1)}, u32[]{:S(2)}) copy-start(bf16[1,768,2048]{2,1,0:T(8,128)(2,1)} %param.28) | copy-start | bytes 9437188
  6.5 21.5 %copy-start.4 = (f32[2048]{0:T(1024)S(1)}, f32[2048]{0:T(1024)}, u32[]{:S(2)}) copy-start(f32[2048]{0:T(1024)} %param.22) | copy-start | bytes 24580
  6.5 62.4 %reduce-scatter.2.cloned.1.call-start = ((), (), s32[]{:S(2)}) async-start(), calls=%async_computation.2 | async-start | bytes 327680 | tf_op jit(solution)/shard_map/reduce_scatter | solution.py:221
  11.1 27.8 %copy-start.7 = (bf16[8,8,512]{2,1,0:T(8,128)(2,1)S(1)}, bf16[8,8,512]{2,1,0:T(8,128)(2,1)}, u32[]{:S(2)}) copy-start(bf16[8,8,512]{2,1,0:T(8,128)(2,1)} %param.21) | copy-start | bytes 196612
  33.1 12.9 %copy-start.1 = (bf16[512,2048]{1,0:T(8,128)(2,1)S(1)}, bf16[512,2048]{1,0:T(8,128)(2,1)}, u32[]{:S(2)}) copy-start(bf16[512,2048]{1,0:T(8,128)(2,1)} %param.24) | copy-start | bytes 6291460
  39.8 7.5 %copy-start.6 = (s32[8,2]{0,1:T(2,128)S(1)}, s32[8,2]{0,1:T(2,128)}, u32[]{:S(2)}) copy-start(s32[8,2]{0,1:T(2,128)} %param.30) | copy-start | bytes 196
  40.1 28.8 %copy-start.2 = (bf16[8,2,2048]{2,1,0:T(2,128)(2,1)S(1)}, bf16[8,2,2048]{2,1,0:T(2,128)(2,1)}, u32[]{:S(2)}) copy-start(bf16[8,2,2048]{2,1,0:T(2,128)(2,1)} %param.20) | copy-start | bytes 196612
  40.1 29.8 %copy-start.5 = (f32[2048]{0:T(1024)S(1)}, f32[2048]{0:T(1024)}, u32[]{:S(2)}) copy-start(f32[2048]{0:T(1024)} %param.25) | copy-start | bytes 24580
  71.7 5.5 %collective-permute-start = (bf16[1,2,2048]{2,1,0:T(2,128)(2,1)S(1)}, bf16[1,2,2048]{2,1,0:T(2,128)(2,1)S(1)}, u32[]{:S(2)}, u32[]{:S(2)}) collective-permute-start(bf16[1,2,2048]{2,1,0:T(2,128)(2,1)S(1)} %get-tuple-element.28), channel_id=1, source_target_pairs={{0,15},{1,0},{2,1},{3,2},{4,3},{5,4},{6,5},{7,6},{8,7},{9,8},{10,9... | collective-permute-start | bytes 24584 | tf_op jit(solution)/shard_map/ppermute | solution.py:24
  71.8 6.7 %collective-permute-start.1 = (bf16[1,2,2048]{2,1,0:T(2,128)(2,1)S(1)}, bf16[1,2,2048]{2,1,0:T(2,128)(2,1)S(1)}, u32[]{:S(2)}, u32[]{:S(2)}) collective-permute-start(bf16[1,2,2048]{2,1,0:T(2,128)(2,1)S(1)} %get-tuple-element.27), channel_id=1, source_target_pairs={{0,14},{1,15},{2,0},{3,1},{4,2},{5,3},{6,4},{7,5},{8,6},{9,7},{10,... | collective-permute-start | bytes 24584 | tf_op jit(solution)/shard_map/ppermute | solution.py:24
  71.9 8.5 %collective-permute-start.2 = (bf16[1,2,2048]{2,1,0:T(2,128)(2,1)S(1)}, bf16[1,2,2048]{2,1,0:T(2,128)(2,1)S(1)}, u32[]{:S(2)}, u32[]{:S(2)}) collective-permute-start(bf16[1,2,2048]{2,1,0:T(2,128)(2,1)S(1)} %get-tuple-element.26), channel_id=1, source_target_pairs={{0,13},{1,14},{2,15},{3,0},{4,1},{5,2},{6,3},{7,4},{8,5},{9,6},{10... | collective-permute-start | bytes 24584 | tf_op jit(solution)/shard_map/ppermute | solution.py:24
  75.0 6.0 %collective-permute-start.3 = (bf16[1,2,2048]{2,1,0:T(2,128)(2,1)S(1)}, bf16[1,2,2048]{2,1,0:T(2,128)(2,1)S(1)}, u32[]{:S(2)}, u32[]{:S(2)}) collective-permute-start(bf16[1,2,2048]{2,1,0:T(2,128)(2,1)S(1)} %get-tuple-element.25), channel_id=1, source_target_pairs={{0,12},{1,13},{2,14},{3,15},{4,0},{5,1},{6,2},{7,3},{8,4},{9,5},{1... | collective-permute-start | bytes 24584 | tf_op jit(solution)/shard_map/ppermute | solution.py:24
  75.1 7.8 %collective-permute-start.4 = (bf16[1,2,2048]{2,1,0:T(2,128)(2,1)S(1)}, bf16[1,2,2048]{2,1,0:T(2,128)(2,1)S(1)}, u32[]{:S(2)}, u32[]{:S(2)}) collective-permute-start(bf16[1,2,2048]{2,1,0:T(2,128)(2,1)S(1)} %get-tuple-element.24), channel_id=1, source_target_pairs={{0,11},{1,12},{2,13},{3,14},{4,15},{5,0},{6,1},{7,2},{8,3},{9,4},{... | collective-permute-start | bytes 24584 | tf_op jit(solution)/shard_map/ppermute | solution.py:24
  77.2 6.5 %collective-permute-start.5 = (bf16[1,2,2048]{2,1,0:T(2,128)(2,1)S(1)}, bf16[1,2,2048]{2,1,0:T(2,128)(2,1)S(1)}, u32[]{:S(2)}, u32[]{:S(2)}) collective-permute-start(bf16[1,2,2048]{2,1,0:T(2,128)(2,1)S(1)} %get-tuple-element.23), channel_id=1, source_target_pairs={{0,10},{1,11},{2,12},{3,13},{4,14},{5,15},{6,0},{7,1},{8,2},{9,3},... | collective-permute-start | bytes 24584 | tf_op jit(solution)/shard_map/ppermute | solution.py:24
  78.5 5.9 %collective-permute-start.6 = (bf16[1,2,2048]{2,1,0:T(2,128)(2,1)S(1)}, bf16[1,2,2048]{2,1,0:T(2,128)(2,1)S(1)}, u32[]{:S(2)}, u32[]{:S(2)}) collective-permute-start(bf16[1,2,2048]{2,1,0:T(2,128)(2,1)S(1)} %get-tuple-element.22), channel_id=1, source_target_pairs={{0,9},{1,10},{2,11},{3,12},{4,13},{5,14},{6,15},{7,0},{8,1},{9,2},... | collective-permute-start | bytes 24584 | tf_op jit(solution)/shard_map/ppermute | solution.py:24
  80.4 4.5 %collective-permute-start.7 = (bf16[1,2,2048]{2,1,0:T(2,128)(2,1)S(1)}, bf16[1,2,2048]{2,1,0:T(2,128)(2,1)S(1)}, u32[]{:S(2)}, u32[]{:S(2)}) collective-permute-start(bf16[1,2,2048]{2,1,0:T(2,128)(2,1)S(1)} %get-tuple-element.21), channel_id=1, source_target_pairs={{0,8},{1,9},{2,10},{3,11},{4,12},{5,13},{6,14},{7,15},{8,0},{9,1},... | collective-permute-start | bytes 24584 | tf_op jit(solution)/shard_map/ppermute | solution.py:24
  81.0 8.3 %collective-permute-start.8 = (bf16[1,2,2048]{2,1,0:T(2,128)(2,1)S(1)}, bf16[1,2,2048]{2,1,0:T(2,128)(2,1)S(1)}, u32[]{:S(2)}, u32[]{:S(2)}) collective-permute-start(bf16[1,2,2048]{2,1,0:T(2,128)(2,1)S(1)} %get-tuple-element.20), channel_id=1, source_target_pairs={{0,7},{1,8},{2,9},{3,10},{4,11},{5,12},{6,13},{7,14},{8,15},{9,0},... | collective-permute-start | bytes 24584 | tf_op jit(solution)/shard_map/ppermute | solution.py:24
  82.9 7.0 %collective-permute-start.9 = (bf16[1,2,2048]{2,1,0:T(2,128)(2,1)S(1)}, bf16[1,2,2048]{2,1,0:T(2,128)(2,1)S(1)}, u32[]{:S(2)}, u32[]{:S(2)}) collective-permute-start(bf16[1,2,2048]{2,1,0:T(2,128)(2,1)S(1)} %get-tuple-element.19), channel_id=1, source_target_pairs={{0,6},{1,7},{2,8},{3,9},{4,10},{5,11},{6,12},{7,13},{8,14},{9,15},... | collective-permute-start | bytes 24584 | tf_op jit(solution)/shard_map/ppermute | solution.py:24
  83.8 6.4 %collective-permute-start.10 = (bf16[1,2,2048]{2,1,0:T(2,128)(2,1)S(1)}, bf16[1,2,2048]{2,1,0:T(2,128)(2,1)S(1)}, u32[]{:S(2)}, u32[]{:S(2)}) collective-permute-start(bf16[1,2,2048]{2,1,0:T(2,128)(2,1)S(1)} %get-tuple-element.18), channel_id=1, source_target_pairs={{0,5},{1,6},{2,7},{3,8},{4,9},{5,10},{6,11},{7,12},{8,13},{9,14},{... | collective-permute-start | bytes 24584 | tf_op jit(solution)/shard_map/ppermute | solution.py:24
  84.4 5.8 %collective-permute-start.11 = (bf16[1,2,2048]{2,1,0:T(2,128)(2,1)S(1)}, bf16[1,2,2048]{2,1,0:T(2,128)(2,1)S(1)}, u32[]{:S(2)}, u32[]{:S(2)}) collective-permute-start(bf16[1,2,2048]{2,1,0:T(2,128)(2,1)S(1)} %get-tuple-element.17), channel_id=1, source_target_pairs={{0,4},{1,5},{2,6},{3,7},{4,8},{5,9},{6,10},{7,11},{8,12},{9,13},{1... | collective-permute-start | bytes 24584 | tf_op jit(solution)/shard_map/ppermute | solution.py:24
  84.8 5.9 %collective-permute-start.12 = (bf16[1,2,2048]{2,1,0:T(2,128)(2,1)S(1)}, bf16[1,2,2048]{2,1,0:T(2,128)(2,1)S(1)}, u32[]{:S(2)}, u32[]{:S(2)}) collective-permute-start(bf16[1,2,2048]{2,1,0:T(2,128)(2,1)S(1)} %get-tuple-element.16), channel_id=1, source_target_pairs={{0,3},{1,4},{2,5},{3,6},{4,7},{5,8},{6,9},{7,10},{8,11},{9,12},{10... | collective-permute-start | bytes 24584 | tf_op jit(solution)/shard_map/ppermute | solution.py:24
  89.4 4.9 %collective-permute-start.13 = (bf16[1,2,2048]{2,1,0:T(2,128)(2,1)S(1)}, bf16[1,2,2048]{2,1,0:T(2,128)(2,1)S(1)}, u32[]{:S(2)}, u32[]{:S(2)}) collective-permute-start(bf16[1,2,2048]{2,1,0:T(2,128)(2,1)S(1)} %get-tuple-element.15), channel_id=1, source_target_pairs={{0,2},{1,3},{2,4},{3,5},{4,6},{5,7},{6,8},{7,9},{8,10},{9,11},{10,... | collective-permute-start | bytes 24584 | tf_op jit(solution)/shard_map/ppermute | solution.py:24
  89.9 5.8 %collective-permute-start.14 = (bf16[1,2,2048]{2,1,0:T(2,128)(2,1)S(1)}, bf16[1,2,2048]{2,1,0:T(2,128)(2,1)S(1)}, u32[]{:S(2)}, u32[]{:S(2)}) collective-permute-start(bf16[1,2,2048]{2,1,0:T(2,128)(2,1)S(1)} %get-tuple-element.14), channel_id=1, source_target_pairs={{0,1},{1,2},{2,3},{3,4},{4,5},{5,6},{6,7},{7,8},{8,9},{9,10},{10,1... | collective-permute-start | bytes 24584 | tf_op jit(solution)/shard_map/ppermute | solution.py:24
  99.3 14.9 %copy-start.3 = (bf16[2,8,2048]{2,1,0:T(8,128)(2,1)S(1)}, bf16[2,8,2048]{2,1,0:T(8,128)(2,1)}, u32[]{:S(2)}) copy-start(bf16[2,8,2048]{2,1,0:T(8,128)(2,1)} %reduce-scatter.2.cloned.1.call-done) | copy-start | bytes 196612
  103.3 10.9 %all-to-all-start = ((bf16[16,2,2048]{2,1,0:T(2,128)(2,1)}), bf16[16,2,2048]{2,1,0:T(2,128)(2,1)S(1)}, u32[]{:S(2)}, u32[]{:S(2)}) async-start(bf16[16,2,2048]{2,1,0:T(2,128)(2,1)} %reshape.387), calls=%async_computation.1 | async-start | bytes 262144 | tf_op jit(solution)/shard_map/all_to_all | solution.py:255
Sparse Core Ops, SparseCore 0:
  47.4 21.5 reduce-scatter.1
